TPU v7x, 512 devices: a whole 4x4x16 slice. The times are simulated.
512 devices in a mesh: gx: 32 (over z, x_lo), gy: 16 (over y, x_hi, core).
Axes of the slice: x: 4 (x_hi: 2, x_lo: 2; x = x_hi * 2 + x_lo), y: 4, z: 16, core: 2. Of those that a mesh axis runs over, the one named last changes fastest.
Arguments:
- field: float32 [256, 128, 192], P('gx', 'gy'), may hold values from -6 to 6
- target: float32 [256, 128, 192], P('gx', 'gy'), may hold values from -6 to 6
- embed_weight: float32 [192, 256], replicated, may hold values from -0.4375 to 0.4375
- norm_gain: float32 [256], replicated, may hold values from 0.5 to 1.5
- attend_weight: float32 [256, 768], replicated, may hold values from -0.375 to 0.375
- output_weight: float32 [256, 256], replicated, may hold values from -0.375 to 0.375
- second_gain: float32 [256], replicated, may hold values from 0.5 to 1.5
- expand_weight: float32 [256, 512], replicated, may hold values from -0.375 to 0.375
- reduce_weight: float32 [512, 256], replicated, may hold values from -0.25 to 0.25
- decode_weight: float32 [256, 192], replicated, may hold values from -0.375 to 0.375
Outputs:
- loss: float32 [], replicated
- field_gradient: float32 [256, 128, 192], P('gx', 'gy')
- embed_gradient: float32 [192, 256], replicated
- norm_gradient: float32 [256], replicated
- attend_gradient: float32 [256, 768], replicated
- output_gradient: float32 [256, 256], replicated
- second_gradient: float32 [256], replicated
- expand_gradient: float32 [256, 512], replicated
- reduce_gradient: float32 [512, 256], replicated
- decode_gradient: float32 [256, 192], replicated
All inputs are finite; a program needn't handle non-finite values.
Results may differ from a plain program's by a relative error of at most 0.0001.
Values sent between devices are 32-bit elements; how exact they have to be, the bound alone decides.
No kernel may reach another device: no remote copies, remote signals or barrier semaphores. Data moves between devices by JAX's collectives and lax.ppermute only.
A program may use at most 128 MiB of HBM per device.

v0:
```python
import jax
import jax.numpy as jnp
from jax import lax
from jax.sharding import PartitionSpec as P

PATCH = 4
HEADS = 8
STEPS = 2
EXACT = lax.Precision.HIGHEST
EPSILON = 1e-06
TIME_STEP = 0.1
VISCOSITY = 0.5


def with_halo(x, sides, width):
    for axis, dim in sides:
        count, length = (lax.axis_size(axis), x.shape[dim])
        up = [(i, (i + 1) % count) for i in range(count)]
        down = [(j, i) for i, j in up]
        last = lax.slice_in_dim(x, length - width, length, axis=dim)
        leading = lax.slice_in_dim(x, 0, width, axis=dim)
        before = lax.ppermute(last, axis, up)
        after = lax.ppermute(leading, axis, down)
        x = jnp.concatenate([before, x, after], axis=dim)
    return x


def matmul(left, right):
    return jnp.dot(left, right, precision=EXACT)


def rms_scale(values, gain):
    power = jnp.mean(values * values, axis=-1, keepdims=True)
    return values * lax.rsqrt(power + EPSILON) * gain


def closure(ext, params):
    (
        embed_weight,
        norm_gain,
        attend_weight,
        output_weight,
        second_gain,
        expand_weight,
        reduce_weight,
        decode_weight,
    ) = params
    wide, tall, depth = ext.shape
    levels = depth // 3
    across, along, upward = (wide // PATCH, tall // PATCH, levels // PATCH)
    patches = ext.reshape(across, PATCH, along, PATCH, 3, upward, PATCH).transpose(
        0, 2, 5, 4, 1, 3, 6
    )
    patches = patches.reshape(across, along, upward, 3 * PATCH * PATCH * PATCH)
    tokens = matmul(patches, embed_weight)
    width = tokens.shape[-1]
    head_size = width // HEADS
    mixed = matmul(rms_scale(tokens, norm_gain), attend_weight)
    inner_x, inner_y = (across - 2, along - 2)
    queries = mixed[1:-1, 1:-1, :, :width].reshape(inner_x, inner_y, upward, HEADS, head_size)
    keyset = mixed[:, :, :, width : 2 * width]
    valset = mixed[:, :, :, 2 * width :]
    offsets = [(shift_x, shift_y) for shift_x in range(3) for shift_y in range(3)]
    keyblock = jnp.concatenate(
        [keyset[sx : sx + inner_x, sy : sy + inner_y] for sx, sy in offsets], axis=2
    )
    valblock = jnp.concatenate(
        [valset[sx : sx + inner_x, sy : sy + inner_y] for sx, sy in offsets], axis=2
    )
    keyblock = keyblock.reshape(inner_x, inner_y, 9 * upward, HEADS, head_size)
    valblock = valblock.reshape(inner_x, inner_y, 9 * upward, HEADS, head_size)
    factor = head_size ** (-0.5)
    scores = jnp.einsum("xyzhe,xywhe->xyhzw", queries, keyblock, precision=EXACT) * factor
    weights = jnp.exp(scores)
    weights = weights / jnp.sum(weights, axis=-1, keepdims=True)
    attended = jnp.einsum("xyhzw,xywhe->xyzhe", weights, valblock, precision=EXACT)
    attended = attended.reshape(inner_x, inner_y, upward, width)
    middle = tokens[1:-1, 1:-1] + matmul(attended, output_weight)
    hidden = jax.nn.silu(matmul(rms_scale(middle, second_gain), expand_weight))
    middle = middle + matmul(hidden, reduce_weight)
    result = matmul(middle, decode_weight).reshape(inner_x, inner_y, upward, 3, PATCH, PATCH, PATCH)
    return result.transpose(0, 4, 1, 5, 3, 2, 6).reshape(inner_x * PATCH, inner_y * PATCH, depth)


def advance(ext, params):
    wide, tall, depth = ext.shape
    levels = depth // 3
    inner = ext[PATCH : wide - PATCH, PATCH : tall - PATCH]
    east = ext[PATCH + 1 : wide - PATCH + 1, PATCH : tall - PATCH]
    west = ext[PATCH - 1 : wide - PATCH - 1, PATCH : tall - PATCH]
    north = ext[PATCH : wide - PATCH, PATCH + 1 : tall - PATCH + 1]
    south = ext[PATCH : wide - PATCH, PATCH - 1 : tall - PATCH - 1]
    level = jnp.arange(depth, dtype=jnp.int32) % levels
    blank = jnp.zeros(inner.shape[:2] + (1,), jnp.float32)
    upper = jnp.where(level == levels - 1, 0.0, jnp.concatenate([inner[:, :, 1:], blank], axis=2))
    lower = jnp.where(level == 0, 0.0, jnp.concatenate([blank, inner[:, :, :-1]], axis=2))
    laplace = east + west + north + south + upper + lower - 6.0 * inner
    speed_x = jnp.concatenate([inner[:, :, 0:levels]] * 3, axis=2)
    speed_y = jnp.concatenate([inner[:, :, levels : 2 * levels]] * 3, axis=2)
    speed_z = jnp.concatenate([inner[:, :, 2 * levels :]] * 3, axis=2)
    carried = 0.5 * (
        speed_x * (east - west) + speed_y * (north - south) + speed_z * (upper - lower)
    )
    return inner + TIME_STEP * (VISCOSITY * laplace - carried + closure(ext, params))


def fold(spread, margin):
    for axis_dim in (0, 1):
        length = spread.shape[axis_dim] - 4 * margin
        middle = lax.slice_in_dim(spread, 2 * margin, 2 * margin + length, axis=axis_dim)
        lowside = lax.slice_in_dim(spread, 0, margin, axis=axis_dim)
        highside = lax.slice_in_dim(spread, length + 3 * margin, length + 4 * margin, axis=axis_dim)
        pad_low = [(0, 0), (0, 0), (0, 0)]
        pad_high = [(0, 0), (0, 0), (0, 0)]
        pad_low[axis_dim] = (0, length - margin)
        pad_high[axis_dim] = (length - margin, 0)
        spread = middle + jnp.pad(lowside, pad_low) + jnp.pad(highside, pad_high)
    return spread


def shards(
    field,
    target,
    embed_weight,
    norm_gain,
    attend_weight,
    output_weight,
    second_gain,
    expand_weight,
    reduce_weight,
    decode_weight,
):
    params = (
        embed_weight,
        norm_gain,
        attend_weight,
        output_weight,
        second_gain,
        expand_weight,
        reduce_weight,
        decode_weight,
    )
    energy = lax.psum(jnp.sum(target * target), ("gx", "gy"))
    current = field
    pullbacks = []
    for step in range(STEPS):
        extended = with_halo(current, (("gx", 0), ("gy", 1)), PATCH)
        current, pullback = jax.vjp(advance, extended, params)
        pullbacks.append(pullback)
    residue = current - target
    cotangent = 2.0 * residue
    gradients = None
    for pullback in reversed(pullbacks):
        back_ext, back_params = pullback(cotangent)
        gradients = (
            back_params if gradients is None else jax.tree.map(jnp.add, gradients, back_params)
        )
        spread = with_halo(back_ext, (("gx", 0), ("gy", 1)), PATCH)
        cotangent = fold(spread, PATCH)
    local_misfit = jnp.sum(residue * residue)
    misfit = lax.psum(local_misfit, ("gx", "gy"))
    summed = lax.psum(tuple(gradients), ("gx", "gy"))
    entries = (
        field.shape[0] * lax.axis_size("gx") * field.shape[1] * lax.axis_size("gy") * field.shape[2]
    )
    scale = jnp.float32(entries) / energy
    loss = misfit / energy
    return (loss, scale * cotangent) + tuple((scale * piece for piece in summed))


def solution(mesh):
    in_specs = (P("gx", "gy", None), P("gx", "gy", None), P(), P(), P(), P(), P(), P(), P(), P())
    out_specs = (P(), P("gx", "gy", None), P(), P(), P(), P(), P(), P(), P(), P())
    return jax.shard_map(shards, mesh=mesh, in_specs=in_specs, out_specs=out_specs, check_vma=False)
```

profile of v0, /device:TPU:1, one launch (start us, length us, event | category | flops | bytes accessed | tf_op | source)
XLA Modules:
  0.0 810.8 jit_solution(4378260794345569212)
XLA Ops:
  8.1 12.9 %collective-permute-start = (f32[4,8,192]{2,1,0:T(8,128)S(1)}, f32[4,8,192]{2,1,0:T(8,128)S(1)}, u32[]{:S(2)}, u32[]{:S(2)}) collective-permute-start(f32[4,8,192]{2,1,0:T(8,128)S(1)} %get-tuple-element.154), channel_id=1, source_target_pairs={{16,0},{32,16},{48,32},{64,48},{80,64},{96,80},{112,96},{128,112},... | collective-permute-start | bytes 73736 | tf_op jit(solution)/shard_map/ppermute | solution.py:23
  20.9 1.9 collective-permute-start.1
  29.2 6.3 collective-permute-start.3
  35.5 1.9 collective-permute-start.2
  38.2 4.5 collective-permute-done.2
  43.3 5.0 reshape.216
  48.4 6.5 copy.78
  54.9 2.7 multiply_reduce_fusion.7
  67.5 2.2 copy.85
  72.3 1.9 collective-permute-start.5
  74.2 5.5 collective-permute-start.4
  80.7 3.0 collective-permute-start.7
  83.7 1.9 collective-permute-start.6
  86.4 4.5 collective-permute-done.6
  90.9 5.0 reshape.224
  96.0 7.0 copy.86
  103.0 3.9 multiply_reduce_fusion.6
  111.8 1.9 fusion.184
  115.0 2.4 copy.88
  117.4 2.3 convolution_bitcast_fusion.10
  124.0 2.2 copy.93
  129.3 2.4 negate_add_fusion.2
  133.4 1.9 copy.94
  138.8 2.1 multiply_reduce_fusion.9
  141.7 2.1 multiply_reduce_fusion.1
  146.6 2.2 fusion.36
  154.1 3.2 fusion.169
  171.2 3.0 fusion.170
  191.8 6.1 copy.118
  198.1 5.1 reshape.239
  203.7 1.9 collective-permute-start.8
  205.6 5.6 collective-permute-start.9
  212.6 3.2 collective-permute-start.10
  215.8 4.0 collective-permute-start.11
  220.4 3.1 collective-permute-done.11
  229.3 2.2 convolution_bitcast_fusion.12
  246.0 3.0 fusion.167
  262.6 3.3 fusion.168
  289.5 2.2 fusion.6
  293.5 6.3 copy.143
  299.8 5.0 reshape.247
  306.0 1.9 collective-permute-start.12
  307.9 5.5 collective-permute-start.13
  313.4 107.6 %all-reduce.72 = (f32[]{:T(128)}, f32[]{:T(128)}, f32[256]{0:T(256)S(1)}, f32[256]{0:T(256)S(1)}) all-reduce(f32[]{:T(128)} %get-tuple-element.141, f32[]{:T(128)} %multiply_reduce_fusion.12, f32[256]{0:T(256)S(1)} %add.385, f32[256]{0:T(256)S(1)} %add.388), channel_id=1, replica_groups=mesh['gx'=32,'gy'=16] {'gx','gy'}, use_global_device_ids=true, to_apply=%region_7.8 | all-reduce | flops 514 | bytes 4112 | tf_op jit(solution)/shard_map/psum | solution.py:161
  422.3 3.5 collective-permute-start.14
  425.9 1.9 collective-permute-start.15
  429.7 3.6 collective-permute-done.15
  434.2 360.8 %all-reduce.76.cloned.1.call-done = (f32[192,256]{1,0:T(8,128)}, f32[256,768]{1,0:T(8,128)}, f32[256,256]{1,0:T(8,128)}, f32[256,512]{1,0:T(8,128)}, f32[512,256]{1,0:T(8,128)}, /*index=5*/f32[256,192]{0,1:T(8,128)}) async-done(((f32[192,256]{1,0:T(8,128)}, f32[256,768]{1,0:T(8,128)}, f32[256,256]{1,0:T(8,128)}, f32[256,512]{1,0:T(8,128)}, f32[512,256]{1,0:T(8,128)}, /*index=5*/f32[256,192]{0,1:T(8,128)}), ...) | async-done | bytes 2490384 | tf_op jit(solution)/shard_map/psum | solution.py:162
  (608 shorter events, 152.3 us)
Async XLA Ops:
  7.2 51.0 %copy-start = (f32[256,768]{1,0:T(8,128)S(1)}, f32[256,768]{1,0:T(8,128)}, u32[]{:S(2)}) copy-start(f32[256,768]{1,0:T(8,128)} %param.14) | copy-start | bytes 2359300
  7.2 787.8 %all-reduce.76.cloned.1.call-start = ((), (), s32[]{:S(2)}) async-start(), calls=%async_computation | async-start | bytes 4980736 | tf_op jit(solution)/shard_map/psum | solution.py:162
  8.1 20.5 %collective-permute-start = (f32[4,8,192]{2,1,0:T(8,128)S(1)}, f32[4,8,192]{2,1,0:T(8,128)S(1)}, u32[]{:S(2)}, u32[]{:S(2)}) collective-permute-start(f32[4,8,192]{2,1,0:T(8,128)S(1)} %get-tuple-element.154), channel_id=1, source_target_pairs={{16,0},{32,16},{48,32},{64,48},{80,64},{96,80},{112,96},{128,112},... | collective-permute-start | bytes 73736 | tf_op jit(solution)/shard_map/ppermute | solution.py:23
  20.9 6.8 collective-permute-start.1
  28.6 14.0 %copy-start.36 = (f32[16,8,192]{2,1,0:T(8,128)}, f32[16,8,192]{2,1,0:T(8,128)S(1)}, u32[]{:S(2)}) copy-start(f32[16,8,192]{2,1,0:T(8,128)S(1)} %constant_dynamic-update-slice_fusion) | copy-start | bytes 294916
  29.2 9.0 %collective-permute-start.3 = (f32[16,4,192]{2,1,0:T(4,128)S(1)}, f32[16,4,192]{2,1,0:T(4,128)S(1)}, u32[]{:S(2)}, u32[]{:S(2)}) collective-permute-start(f32[16,4,192]{2,1,0:T(4,128)S(1)} %get-tuple-element.122), channel_id=1, source_target_pairs={{0,1},{1,2},{2,3},{3,4},{4,5},{5,6},{6,7},{7,8},{8,9},{9,10},{10,1... | collective-permute-start | bytes 147464 | tf_op jit(solution)/shard_map/ppermute | solution.py:22
  35.5 7.1 collective-permute-start.2
  37.5 33.5 %copy-start.191 = (pred[192]{0:T(512)(128)(4,1)}, pred[192]{0:T(512)(128)(4,1)S(1)}, u32[]{:S(2)}) copy-start(pred[192]{0:T(512)(128)(4,1)S(1)} %get-tuple-element.177) | copy-start | bytes 580
  37.5 33.5 %copy-start.196 = (pred[192]{0:T(512)(128)(4,1)}, pred[192]{0:T(512)(128)(4,1)S(1)}, u32[]{:S(2)}) copy-start(pred[192]{0:T(512)(128)(4,1)S(1)} %get-tuple-element.176) | copy-start | bytes 580
  72.3 8.1 %collective-permute-start.5 = (f32[4,8,192]{2,1,0:T(8,128)S(1)}, f32[4,8,192]{2,1,0:T(8,128)S(1)}, u32[]{:S(2)}, u32[]{:S(2)}) collective-permute-start(f32[4,8,192]{2,1,0:T(8,128)S(1)} %get-tuple-element.147), channel_id=1, source_target_pairs={{0,16},{16,32},{32,48},{48,64},{64,80},{80,96},{96,112},{112,128},... | collective-permute-start | bytes 73736 | tf_op jit(solution)/shard_map/ppermute | solution.py:22
  74.2 6.5 collective-permute-start.4
  80.4 15.5 %copy-start.111 = (f32[4,8,192]{2,1,0:T(8,128)}, f32[4,8,192]{2,1,0:T(8,128)S(1)}, u32[]{:S(2)}) copy-start(f32[4,8,192]{2,1,0:T(8,128)S(1)} %collective-permute-done.5) | copy-start | bytes 73732
  80.7 15.3 %copy-start.113 = (f32[4,8,192]{2,1,0:T(8,128)}, f32[4,8,192]{2,1,0:T(8,128)S(1)}, u32[]{:S(2)}) copy-start(f32[4,8,192]{2,1,0:T(8,128)S(1)} %collective-permute-done.4) | copy-start | bytes 73732
  80.7 5.6 collective-permute-start.7
  83.7 7.1 collective-permute-start.6
  86.4 9.6 %copy-start.102 = (f32[16,4,192]{2,1,0:T(4,128)}, f32[16,4,192]{2,1,0:T(4,128)S(1)}, u32[]{:S(2)}) copy-start(f32[16,4,192]{2,1,0:T(4,128)S(1)} %collective-permute-done.7) | copy-start | bytes 147460
  160.3 9.3 %copy-start.46 = (f32[2,2,16,256]{2,3,1,0:T(8,128)S(1)}, f32[2,2,16,256]{2,3,1,0:T(8,128)}, u32[]{:S(2)}) copy-start(f32[2,2,16,256]{2,3,1,0:T(8,128)} %get-tuple-element.57) | copy-start | bytes 196612
  162.2 8.2 %copy-start.45 = (f32[2,2,16,256]{2,3,1,0:T(8,128)S(1)}, f32[2,2,16,256]{2,3,1,0:T(8,128)}, u32[]{:S(2)}) copy-start(f32[2,2,16,256]{2,3,1,0:T(8,128)} %get-tuple-element.58) | copy-start | bytes 196612
  176.0 9.4 %copy-start.49 = (f32[2,2,16,256]{2,3,1,0:T(8,128)S(1)}, f32[2,2,16,256]{2,3,1,0:T(8,128)}, u32[]{:S(2)}) copy-start(f32[2,2,16,256]{2,3,1,0:T(8,128)} %get-tuple-element.65) | copy-start | bytes 196612
  177.9 8.3 %copy-start.47 = (f32[2,2,16,256]{2,3,1,0:T(8,128)S(1)}, f32[2,2,16,256]{2,3,1,0:T(8,128)}, u32[]{:S(2)}) copy-start(f32[2,2,16,256]{2,3,1,0:T(8,128)} %get-tuple-element.66) | copy-start | bytes 196612
  203.2 16.6 %copy-start.155 = (f32[2,2,8,16]{3,2,1,0:T(8,128)S(1)}, f32[2,2,8,16]{3,2,1,0:T(8,128)}, u32[]{:S(2)}) copy-start(f32[2,2,8,16]{3,2,1,0:T(8,128)} %copy-done.154) | copy-start | bytes 6148
  203.5 20.1 %copy-start.194 = (pred[8]{0:T(512)(128)(4,1)S(1)}, pred[8]{0:T(512)(128)(4,1)}, u32[]{:S(2)}) copy-start(pred[8]{0:T(512)(128)(4,1)} %constant.73.clone.1) | copy-start | bytes 28
  203.7 20.0 %copy-start.108 = (f32[8,8,64]{2,1,0:T(8,128)S(1)}, f32[8,8,64]{2,1,0:T(8,128)}, u32[]{:S(2)}) copy-start(f32[8,8,64]{2,1,0:T(8,128)} %get-tuple-element.152) | copy-start | bytes 49156
  203.7 8.3 %collective-permute-start.8 = (f32[4,16,192]{2,1,0:T(8,128)S(1)}, f32[4,16,192]{2,1,0:T(8,128)S(1)}, u32[]{:S(2)}, u32[]{:S(2)}) collective-permute-start(f32[4,16,192]{2,1,0:T(8,128)S(1)} %get-tuple-element.112), channel_id=1, source_target_pairs={{0,16},{16,32},{32,48},{48,64},{64,80},{80,96},{96,112},{112,128},... | collective-permute-start | bytes 147464 | tf_op jit(solution)/shard_map/ppermute | solution.py:22
  205.6 6.9 collective-permute-start.9
  211.9 12.5 %copy-start.37 = (f32[16,8,192]{2,1,0:T(8,128)S(1)}, f32[16,8,192]{2,1,0:T(8,128)}, u32[]{:S(2)}) copy-start(f32[16,8,192]{2,1,0:T(8,128)} %copy-done.36) | copy-start | bytes 294916
  211.9 12.5 %copy-start.90 = (f32[8,8,191]{2,1,0:T(8,128)S(1)}, f32[8,8,191]{2,1,0:T(8,128)}, u32[]{:S(2)}) copy-start(f32[8,8,191]{2,1,0:T(8,128)} %get-tuple-element.149) | copy-start | bytes 146692
  211.9 12.5 %copy-start.91 = (f32[8,8,191]{2,1,0:T(8,128)S(1)}, f32[8,8,191]{2,1,0:T(8,128)}, u32[]{:S(2)}) copy-start(f32[8,8,191]{2,1,0:T(8,128)} %get-tuple-element.150) | copy-start | bytes 146692
  211.9 12.5 %copy-start.95 = (f32[16,4,192]{2,1,0:T(4,128)S(1)}, f32[16,4,192]{2,1,0:T(4,128)}, u32[]{:S(2)}) copy-start(f32[16,4,192]{2,1,0:T(4,128)} %copy-done.94) | copy-start | bytes 147460
  211.9 12.5 %copy-start.97 = (f32[16,4,192]{2,1,0:T(4,128)S(1)}, f32[16,4,192]{2,1,0:T(4,128)}, u32[]{:S(2)}) copy-start(f32[16,4,192]{2,1,0:T(4,128)} %copy-done.96) | copy-start | bytes 147460
  211.9 12.5 %copy-start.124 = (f32[4,8,192]{2,1,0:T(8,128)S(1)}, f32[4,8,192]{2,1,0:T(8,128)}, u32[]{:S(2)}) copy-start(f32[4,8,192]{2,1,0:T(8,128)} %copy-done.123) | copy-start | bytes 73732
  212.0 12.5 %copy-start.126 = (f32[4,8,192]{2,1,0:T(8,128)S(1)}, f32[4,8,192]{2,1,0:T(8,128)}, u32[]{:S(2)}) copy-start(f32[4,8,192]{2,1,0:T(8,128)} %copy-done.125) | copy-start | bytes 73732
  212.0 12.5 %copy-start.128 = (f32[8,8,64]{2,1,0:T(8,128)S(1)}, f32[8,8,64]{2,1,0:T(8,128)}, u32[]{:S(2)}) copy-start(f32[8,8,64]{2,1,0:T(8,128)} %get-tuple-element.153) | copy-start | bytes 49156
  212.0 12.5 %copy-start.197 = (pred[192]{0:T(512)(128)(4,1)S(1)}, pred[192]{0:T(512)(128)(4,1)}, u32[]{:S(2)}) copy-start(pred[192]{0:T(512)(128)(4,1)} %copy-done.196) | copy-start | bytes 580
  212.6 7.8 collective-permute-start.10
  215.8 7.7 collective-permute-start.11
  250.9 9.3 %copy-start.50 = (f32[2,2,16,256]{2,3,1,0:T(8,128)S(1)}, f32[2,2,16,256]{2,3,1,0:T(8,128)}, u32[]{:S(2)}) copy-start(f32[2,2,16,256]{2,3,1,0:T(8,128)} %get-tuple-element.38) | copy-start | bytes 196612
  265.8 9.4 %copy-start.52 = (f32[2,2,16,256]{2,3,1,0:T(8,128)S(1)}, f32[2,2,16,256]{2,3,1,0:T(8,128)}, u32[]{:S(2)}) copy-start(f32[2,2,16,256]{2,3,1,0:T(8,128)} %get-tuple-element.46) | copy-start | bytes 196612
  267.7 8.3 %copy-start.51 = (f32[2,2,16,256]{2,3,1,0:T(8,128)S(1)}, f32[2,2,16,256]{2,3,1,0:T(8,128)}, u32[]{:S(2)}) copy-start(f32[2,2,16,256]{2,3,1,0:T(8,128)} %get-tuple-element.47) | copy-start | bytes 196612
  305.2 8.2 %copy-start.198 = (f32[256]{0:T(256)S(1)}, f32[256]{0:T(256)}, u32[]{:S(2)}) copy-start(f32[256]{0:T(256)} %get-tuple-element.16) | copy-start | bytes 3076
  305.2 8.2 %copy-start.200 = (f32[256]{0:T(256)S(1)}, f32[256]{0:T(256)}, u32[]{:S(2)}) copy-start(f32[256]{0:T(256)} %get-tuple-element.14) | copy-start | bytes 3076
  305.2 8.2 %copy-start.199 = (f32[256]{0:T(256)S(1)}, f32[256]{0:T(256)}, u32[]{:S(2)}) copy-start(f32[256]{0:T(256)} %get-tuple-element.12) | copy-start | bytes 3076
  305.2 8.2 %copy-start.201 = (f32[256]{0:T(256)S(1)}, f32[256]{0:T(256)}, u32[]{:S(2)}) copy-start(f32[256]{0:T(256)} %get-tuple-element.10) | copy-start | bytes 3076
  305.2 128.2 %copy-start.195 = (pred[8]{0:T(512)(128)(4,1)S(1)}, pred[8]{0:T(512)(128)(4,1)}, u32[]{:S(2)}) copy-start(pred[8]{0:T(512)(128)(4,1)} %constant.73.clone.1) | copy-start | bytes 28
  306.0 116.3 %collective-permute-start.12 = (f32[4,16,192]{2,1,0:T(8,128)S(1)}, f32[4,16,192]{2,1,0:T(8,128)S(1)}, u32[]{:S(2)}, u32[]{:S(2)}) collective-permute-start(f32[4,16,192]{2,1,0:T(8,128)S(1)} %get-tuple-element.110), channel_id=1, source_target_pairs={{0,16},{16,32},{32,48},{48,64},{64,80},{80,96},{96,112},{112,128},... | collective-permute-start | bytes 147464 | tf_op jit(solution)/shard_map/ppermute | solution.py:22
  307.9 114.4 %collective-permute-start.13 = (f32[4,16,192]{2,1,0:T(8,128)S(1)}, f32[4,16,192]{2,1,0:T(8,128)S(1)}, u32[]{:S(2)}, u32[]{:S(2)}) collective-permute-start(f32[4,16,192]{2,1,0:T(8,128)S(1)} %get-tuple-element.111), channel_id=1, source_target_pairs={{16,0},{32,16},{48,32},{64,48},{80,64},{96,80},{112,96},{128,112},... | collective-permute-start | bytes 147464 | tf_op jit(solution)/shard_map/ppermute | solution.py:23
  422.3 7.4 collective-permute-start.14
  425.9 7.4 collective-permute-start.15
  (173 other events, 568.2 us)
Sparse Core Ops, SparseCore 0:
  305.3 489.6 all-reduce.75
where the time goes:
time: 823 us; the launch traced here: 811 us
  waiting for transfers between devices  379 us (46%)
  local copies, waits for them, and re-layouts  147 us (18%)
  blocking collectives  108 us (13%)
  matrix products  67.6 us (8%)
  starting transfers between devices  63 us (8%)
  other arithmetic  26.2 us (3%)
  between operations  20.3 us (2%)
    psum x1, waiting for transfers between devices, shards(): summed = lax.psum(tuple(gradients), ('gx', 'gy'))  361 us
    psum x1, blocking collectives, shards(): misfit = lax.psum(local_misfit, ('gx', 'gy'))  108 us
    unnamed x462, local copies, waits for them, and re-layouts  58.7 us
    dot_general x36, matrix products, matmul(): return jnp.dot(left, right, precision=EXACT)  49.2 us
    ppermute x8, starting transfers between devices, with_halo(): after = lax.ppermute(leading, axis, down)  39.2 us
    transpose x4, local copies, waits for them, and re-layouts, closure(): ext.reshape(across, PATCH, along, PATCH, 3, upward, PATCH)  25.9 us
    ppermute x8, starting transfers between devices, with_halo(): before = lax.ppermute(last, axis, up)  23.7 us
    reshape x4, local copies, waits for them, and re-layouts, closure(): ext.reshape(across, PATCH, along, PATCH, 3, upward, PATCH)  20.2 us
  transfers between devices with their start and end apart: 17, of which 8 were waited for; matrix products, arithmetic and copies ran while one was open for 1% of the time, Pallas kernels for 0%

commit v1 on v0

--- a/solution.py
+++ b/solution.py
@@ -159,7 +159,7 @@
         cotangent = fold(spread, PATCH)
     local_misfit = jnp.sum(residue * residue)
     misfit = lax.psum(local_misfit, ("gx", "gy"))
-    summed = lax.psum(tuple(gradients), ("gx", "gy"))
+    summed = lax.psum(lax.psum(tuple(gradients), "gy"), "gx")
     entries = (
         field.shape[0] * lax.axis_size("gx") * field.shape[1] * lax.axis_size("gy") * field.shape[2]
     )

time: 823 us -> 760 us (0.923)
  the two profiles are of different devices: /device:TPU:1 before, /device:TPU:16 now
where the time goes in v1:
time: 760 us; the launch traced here: 748 us
  waiting for transfers between devices  236 us (31%)
  blocking collectives  198 us (26%)
  local copies, waits for them, and re-layouts  147 us (19%)
  matrix products  65.8 us (9%)
  starting transfers between devices  53.6 us (7%)
  other arithmetic  27 us (4%)
  between operations  20.4 us (3%)
    psum x2, waiting for transfers between devices, shards(): summed = lax.psum(lax.psum(tuple(gradients), 'gy'), 'gx')  206 us
    psum x1, blocking collectives, shards(): misfit = lax.psum(local_misfit, ('gx', 'gy'))  103 us
    psum x2, blocking collectives, shards(): summed = lax.psum(lax.psum(tuple(gradients), 'gy'), 'gx')  95.4 us
    unnamed x462, local copies, waits for them, and re-layouts  60.1 us
    dot_general x36, matrix products, matmul(): return jnp.dot(left, right, precision=EXACT)  48.3 us
    ppermute x8, starting transfers between devices, with_halo(): after = lax.ppermute(leading, axis, down)  32.2 us
    ppermute x8, waiting for transfers between devices, with_halo(): before = lax.ppermute(last, axis, up)  29.7 us
    transpose x4, local copies, waits for them, and re-layouts, closure(): ext.reshape(across, PATCH, along, PATCH, 3, upward, PATCH)  26 us
  transfers between devices with their start and end apart: 18, of which 9 were waited for; matrix products, arithmetic and copies ran while one was open for 3% of the time, Pallas kernels for 0%

profile of v1, /device:TPU:16, one launch (start us, length us, event | category | flops | bytes accessed | tf_op | source)
XLA Modules:
  0.0 748.4 jit_solution(15056238327043706316)
XLA Ops:
  8.1 3.4 collective-permute-start.1
  11.5 10.9 %collective-permute-start = (f32[4,8,192]{2,1,0:T(8,128)S(1)}, f32[4,8,192]{2,1,0:T(8,128)S(1)}, u32[]{:S(2)}, u32[]{:S(2)}) collective-permute-start(f32[4,8,192]{2,1,0:T(8,128)S(1)} %get-tuple-element.162), channel_id=1, source_target_pairs={{16,0},{32,16},{48,32},{64,48},{80,64},{96,80},{112,96},{128,112},... | collective-permute-start | bytes 73736 | tf_op jit(solution)/shard_map/ppermute | solution.py:23
  27.0 3.7 collective-permute-start.2
  33.3 5.4 collective-permute-done.3
  39.3 5.1 reshape.216
  44.4 6.5 copy.78
  50.9 2.7 multiply_reduce_fusion.7
  59.6 2.4 convolution_bitcast_fusion.11
  65.7 2.2 copy.85
  70.5 3.0 collective-permute-start.4
  73.5 2.8 collective-permute-start.5
  77.0 4.4 collective-permute-done.5
  83.4 2.4 collective-permute-start.7
  86.5 4.9 collective-permute-done.7
  91.5 5.1 reshape.224
  96.5 7.0 copy.86
  103.5 3.9 multiply_reduce_fusion.6
  110.2 2.4 copy.88
  121.9 2.2 copy.93
  127.2 2.4 negate_add_fusion.2
  141.0 2.3 multiply_reduce_fusion.1
  145.8 2.2 fusion.36
  152.6 3.2 fusion.170
  170.3 2.8 fusion.169
  187.4 2.2 multiply_reduce_fusion.3
  191.1 6.3 copy.118
  197.5 5.1 reshape.239
  203.1 2.1 collective-permute-start.9
  205.3 3.8 collective-permute-start.8
  209.8 3.9 collective-permute-done.8
  215.7 2.6 collective-permute-start.10
  218.9 5.1 collective-permute-done.10
  232.2 2.0 multiply_reduce_fusion.8
  242.0 3.0 fusion.168
  258.5 2.7 fusion.167
  274.1 2.2 multiply_reduce_fusion.2
  281.8 2.2 fusion.6
  291.9 102.7 %all-reduce.72 = (f32[]{:T(128)}, f32[]{:T(128)}) all-reduce(f32[]{:T(128)} %get-tuple-element.149, f32[]{:T(128)} %multiply_reduce_fusion.12), channel_id=1, replica_groups=mesh['gx'=32,'gy'=16] {'gx','gy'}, use_global_device_ids=true, to_apply=%region_7.8 | all-reduce | flops 2 | bytes 16 | tf_op jit(solution)/shard_map/psum | solution.py:161
  398.1 6.3 copy.143
  404.4 5.0 reshape.247
  409.5 35.4 %all-reduce.82.cloned.1.call-done = (f32[192,256]{1,0:T(8,128)}, f32[256,768]{1,0:T(8,128)}, f32[256,256]{1,0:T(8,128)}, f32[256,512]{1,0:T(8,128)}, f32[512,256]{1,0:T(8,128)}, /*index=5*/f32[256,192]{0,1:T(8,128)}) async-done(((f32[192,256]{1,0:T(8,128)}, f32[256,768]{1,0:T(8,128)}, f32[256,256]{1,0:T(8,128)}, f32[256,512]{1,0:T(8,128)}, f32[512,256]{1,0:T(8,128)}, /*index=5*/f32[256,192]{0,1:T(8,128)}), ...) | async-done | bytes 2490384 | tf_op jit(solution)/shard_map/psum | solution.py:162
  446.0 6.8 collective-permute-start.13
  454.8 31.7 %all-reduce.75 = (f32[256]{0:T(256)S(1)}, f32[256]{0:T(256)S(1)}) all-reduce(f32[256]{0:T(256)S(1)} %add.401, f32[256]{0:T(256)S(1)} %add.404), channel_id=1, replica_groups=mesh['gx'=32,'gy'=16] {'gy'}, use_global_device_ids=true, to_apply=%region_20.21 | all-reduce | flops 512 | bytes 4096 | tf_op jit(solution)/shard_map/psum | solution.py:162
  486.5 63.7 %all-reduce.73 = (f32[256]{0:T(256)S(1)}, f32[256]{0:T(256)S(1)}) all-reduce(f32[256]{0:T(256)S(1)} %get-tuple-element.28, f32[256]{0:T(256)S(1)} %get-tuple-element.29), channel_id=1, replica_groups=mesh['gx'=32,'gy'=16] {'gx'}, use_global_device_ids=true, to_apply=%region_21.22 | all-reduce | flops 512 | bytes 4096 | tf_op jit(solution)/shard_map/psum | solution.py:162
  552.8 2.4 collective-permute-start.14
  555.7 6.1 collective-permute-done.14
  562.8 170.6 %all-reduce.80.cloned.1.call-done = (f32[192,256]{1,0:T(8,128)}, f32[256,768]{1,0:T(8,128)}, f32[256,256]{1,0:T(8,128)}, f32[256,512]{1,0:T(8,128)}, f32[512,256]{1,0:T(8,128)}, /*index=5*/f32[256,192]{0,1:T(8,128)}) async-done(((f32[192,256]{1,0:T(8,128)}, f32[256,768]{1,0:T(8,128)}, f32[256,256]{1,0:T(8,128)}, f32[256,512]{1,0:T(8,128)}, f32[512,256]{1,0:T(8,128)}, /*index=5*/f32[256,192]{0,1:T(8,128)}), ...) | async-done | bytes 2490384 | tf_op jit(solution)/shard_map/psum | solution.py:162
  735.0 2.1 broadcast_multiply_fusion
  (613 shorter events, 159.2 us)
Async XLA Ops:
  7.2 47.1 %copy-start = (f32[256,768]{1,0:T(8,128)S(1)}, f32[256,768]{1,0:T(8,128)}, u32[]{:S(2)}) copy-start(f32[256,768]{1,0:T(8,128)} %param.14) | copy-start | bytes 2359300
  7.2 437.7 %all-reduce.82.cloned.1.call-start = ((), (), s32[]{:S(2)}) async-start(), calls=%async_computation.1 | async-start | bytes 4980736 | tf_op jit(solution)/shard_map/psum | solution.py:162
  8.1 17.4 %collective-permute-start.1 = (f32[4,8,192]{2,1,0:T(8,128)S(1)}, f32[4,8,192]{2,1,0:T(8,128)S(1)}, u32[]{:S(2)}, u32[]{:S(2)}) collective-permute-start(f32[4,8,192]{2,1,0:T(8,128)S(1)} %get-tuple-element.163), channel_id=1, source_target_pairs={{0,16},{16,32},{32,48},{48,64},{64,80},{80,96},{96,112},{112,128},... | collective-permute-start | bytes 73736 | tf_op jit(solution)/shard_map/ppermute | solution.py:22
  11.5 14.9 %collective-permute-start = (f32[4,8,192]{2,1,0:T(8,128)S(1)}, f32[4,8,192]{2,1,0:T(8,128)S(1)}, u32[]{:S(2)}, u32[]{:S(2)}) collective-permute-start(f32[4,8,192]{2,1,0:T(8,128)S(1)} %get-tuple-element.162), channel_id=1, source_target_pairs={{16,0},{32,16},{48,32},{64,48},{80,64},{96,80},{112,96},{128,112},... | collective-permute-start | bytes 73736 | tf_op jit(solution)/shard_map/ppermute | solution.py:23
  26.4 12.3 %copy-start.36 = (f32[16,8,192]{2,1,0:T(8,128)}, f32[16,8,192]{2,1,0:T(8,128)S(1)}, u32[]{:S(2)}) copy-start(f32[16,8,192]{2,1,0:T(8,128)S(1)} %constant_dynamic-update-slice_fusion) | copy-start | bytes 294916
  27.0 6.3 collective-permute-start.2
  30.6 8.0 %collective-permute-start.3 = (f32[16,4,192]{2,1,0:T(4,128)S(1)}, f32[16,4,192]{2,1,0:T(4,128)S(1)}, u32[]{:S(2)}, u32[]{:S(2)}) collective-permute-start(f32[16,4,192]{2,1,0:T(4,128)S(1)} %get-tuple-element.130), channel_id=1, source_target_pairs={{0,1},{1,2},{2,3},{3,4},{4,5},{5,6},{6,7},{7,8},{8,9},{9,10},{10,1... | collective-permute-start | bytes 147464 | tf_op jit(solution)/shard_map/ppermute | solution.py:22
  32.6 36.6 %copy-start.191 = (pred[192]{0:T(512)(128)(4,1)}, pred[192]{0:T(512)(128)(4,1)S(1)}, u32[]{:S(2)}) copy-start(pred[192]{0:T(512)(128)(4,1)S(1)} %get-tuple-element.185) | copy-start | bytes 580
  32.6 36.6 %copy-start.196 = (pred[192]{0:T(512)(128)(4,1)}, pred[192]{0:T(512)(128)(4,1)S(1)}, u32[]{:S(2)}) copy-start(pred[192]{0:T(512)(128)(4,1)S(1)} %get-tuple-element.184) | copy-start | bytes 580
  70.5 6.6 collective-permute-start.4
  73.5 7.9 %collective-permute-start.5 = (f32[4,8,192]{2,1,0:T(8,128)S(1)}, f32[4,8,192]{2,1,0:T(8,128)S(1)}, u32[]{:S(2)}, u32[]{:S(2)}) collective-permute-start(f32[4,8,192]{2,1,0:T(8,128)S(1)} %get-tuple-element.155), channel_id=1, source_target_pairs={{0,16},{16,32},{32,48},{48,64},{64,80},{80,96},{96,112},{112,128},... | collective-permute-start | bytes 73736 | tf_op jit(solution)/shard_map/ppermute | solution.py:22
  77.0 19.5 %copy-start.103 = (f32[4,8,192]{2,1,0:T(8,128)}, f32[4,8,192]{2,1,0:T(8,128)S(1)}, u32[]{:S(2)}) copy-start(f32[4,8,192]{2,1,0:T(8,128)S(1)} %collective-permute-done.4) | copy-start | bytes 73732
  81.4 15.1 %copy-start.104 = (f32[4,8,192]{2,1,0:T(8,128)}, f32[4,8,192]{2,1,0:T(8,128)S(1)}, u32[]{:S(2)}) copy-start(f32[4,8,192]{2,1,0:T(8,128)S(1)} %collective-permute-done.5) | copy-start | bytes 73732
  81.5 5.0 collective-permute-start.6
  83.4 8.0 %collective-permute-start.7 = (f32[16,4,192]{2,1,0:T(4,128)S(1)}, f32[16,4,192]{2,1,0:T(4,128)S(1)}, u32[]{:S(2)}, u32[]{:S(2)}) collective-permute-start(f32[16,4,192]{2,1,0:T(4,128)S(1)} %get-tuple-element.128), channel_id=1, source_target_pairs={{0,1},{1,2},{2,3},{3,4},{4,5},{5,6},{6,7},{7,8},{8,9},{9,10},{10,1... | collective-permute-start | bytes 147464 | tf_op jit(solution)/shard_map/ppermute | solution.py:22
  86.5 10.0 %copy-start.98 = (f32[16,4,192]{2,1,0:T(4,128)}, f32[16,4,192]{2,1,0:T(4,128)S(1)}, u32[]{:S(2)}) copy-start(f32[16,4,192]{2,1,0:T(4,128)S(1)} %collective-permute-done.6) | copy-start | bytes 147460
  202.6 15.7 %copy-start.156 = (f32[2,2,8,16]{3,2,1,0:T(8,128)S(1)}, f32[2,2,8,16]{3,2,1,0:T(8,128)}, u32[]{:S(2)}) copy-start(f32[2,2,8,16]{3,2,1,0:T(8,128)} %copy-done.155) | copy-start | bytes 6148
  202.8 21.3 %copy-start.194 = (pred[8]{0:T(512)(128)(4,1)S(1)}, pred[8]{0:T(512)(128)(4,1)}, u32[]{:S(2)}) copy-start(pred[8]{0:T(512)(128)(4,1)} %constant.73.clone.1) | copy-start | bytes 28
  203.0 21.2 %copy-start.102 = (f32[8,8,64]{2,1,0:T(8,128)S(1)}, f32[8,8,64]{2,1,0:T(8,128)}, u32[]{:S(2)}) copy-start(f32[8,8,64]{2,1,0:T(8,128)} %get-tuple-element.160) | copy-start | bytes 49156
  203.1 6.7 collective-permute-start.9
  205.2 19.8 %copy-start.37 = (f32[16,8,192]{2,1,0:T(8,128)S(1)}, f32[16,8,192]{2,1,0:T(8,128)}, u32[]{:S(2)}) copy-start(f32[16,8,192]{2,1,0:T(8,128)} %copy-done.36) | copy-start | bytes 294916
  205.2 19.8 %copy-start.86 = (f32[8,8,191]{2,1,0:T(8,128)S(1)}, f32[8,8,191]{2,1,0:T(8,128)}, u32[]{:S(2)}) copy-start(f32[8,8,191]{2,1,0:T(8,128)} %get-tuple-element.157) | copy-start | bytes 146692
  205.2 19.8 %copy-start.87 = (f32[8,8,191]{2,1,0:T(8,128)S(1)}, f32[8,8,191]{2,1,0:T(8,128)}, u32[]{:S(2)}) copy-start(f32[8,8,191]{2,1,0:T(8,128)} %get-tuple-element.158) | copy-start | bytes 146692
  205.2 19.8 %copy-start.89 = (f32[16,4,192]{2,1,0:T(4,128)S(1)}, f32[16,4,192]{2,1,0:T(4,128)}, u32[]{:S(2)}) copy-start(f32[16,4,192]{2,1,0:T(4,128)} %copy-done.88) | copy-start | bytes 147460
  205.2 19.8 %copy-start.91 = (f32[16,4,192]{2,1,0:T(4,128)S(1)}, f32[16,4,192]{2,1,0:T(4,128)}, u32[]{:S(2)}) copy-start(f32[16,4,192]{2,1,0:T(4,128)} %copy-done.90) | copy-start | bytes 147460
  205.2 19.8 %copy-start.116 = (f32[4,8,192]{2,1,0:T(8,128)S(1)}, f32[4,8,192]{2,1,0:T(8,128)}, u32[]{:S(2)}) copy-start(f32[4,8,192]{2,1,0:T(8,128)} %copy-done.115) | copy-start | bytes 73732
  205.2 19.8 %copy-start.118 = (f32[4,8,192]{2,1,0:T(8,128)S(1)}, f32[4,8,192]{2,1,0:T(8,128)}, u32[]{:S(2)}) copy-start(f32[4,8,192]{2,1,0:T(8,128)} %copy-done.117) | copy-start | bytes 73732
  205.3 19.8 %copy-start.120 = (f32[8,8,64]{2,1,0:T(8,128)S(1)}, f32[8,8,64]{2,1,0:T(8,128)}, u32[]{:S(2)}) copy-start(f32[8,8,64]{2,1,0:T(8,128)} %get-tuple-element.161) | copy-start | bytes 49156
  205.3 19.8 %copy-start.197 = (pred[192]{0:T(512)(128)(4,1)S(1)}, pred[192]{0:T(512)(128)(4,1)}, u32[]{:S(2)}) copy-start(pred[192]{0:T(512)(128)(4,1)} %copy-done.196) | copy-start | bytes 580
  205.3 8.4 %collective-permute-start.8 = (f32[4,16,192]{2,1,0:T(8,128)S(1)}, f32[4,16,192]{2,1,0:T(8,128)S(1)}, u32[]{:S(2)}, u32[]{:S(2)}) collective-permute-start(f32[4,16,192]{2,1,0:T(8,128)S(1)} %get-tuple-element.120), channel_id=1, source_target_pairs={{0,16},{16,32},{32,48},{48,64},{64,80},{80,96},{96,112},{112,128},... | collective-permute-start | bytes 147464 | tf_op jit(solution)/shard_map/ppermute | solution.py:22
  213.7 5.2 collective-permute-start.11
  215.7 8.3 %collective-permute-start.10 = (f32[24,4,192]{2,1,0:T(4,128)S(1)}, f32[24,4,192]{2,1,0:T(4,128)S(1)}, u32[]{:S(2)}, u32[]{:S(2)}) collective-permute-start(f32[24,4,192]{2,1,0:T(4,128)S(1)} %get-tuple-element.116), channel_id=1, source_target_pairs={{0,1},{1,2},{2,3},{3,4},{4,5},{5,6},{6,7},{7,8},{8,9},{9,10},{10,1... | collective-permute-start | bytes 221192 | tf_op jit(solution)/shard_map/ppermute | solution.py:22
  289.9 106.7 %copy-start.35 = (f32[192,256]{1,0:T(8,128)S(1)}, f32[192,256]{1,0:T(8,128)}, u32[]{:S(2)}) copy-start(f32[192,256]{1,0:T(8,128)} %param.12) | copy-start | bytes 589828
  289.9 106.7 %copy-start.175 = (f32[256]{0:T(256)S(1)}, f32[256]{0:T(256)}, u32[]{:S(2)}) copy-start(f32[256]{0:T(256)} %param.13) | copy-start | bytes 3076
  291.3 442.1 %all-reduce.80.cloned.1.call-start = ((), (), s32[]{:S(2)}) async-start(), calls=%async_computation | async-start | bytes 4980736 | tf_op jit(solution)/shard_map/psum | solution.py:162
  409.4 35.6 %copy-start.110 = (f32[8,8,192]{2,1,0:T(8,128)S(1)}, f32[8,8,192]{2,1,0:T(8,128)}, u32[]{:S(2)}) copy-start(f32[8,8,192]{2,1,0:T(8,128)} %get-tuple-element.138) | copy-start | bytes 147460
  409.4 35.7 %copy-start.109 = (f32[8,8,192]{2,1,0:T(8,128)S(1)}, f32[8,8,192]{2,1,0:T(8,128)}, u32[]{:S(2)}) copy-start(f32[8,8,192]{2,1,0:T(8,128)} %get-tuple-element.139) | copy-start | bytes 147460
  409.4 35.8 %copy-start.82 = (f32[8,8,192]{2,1,0:T(8,128)S(1)}, f32[8,8,192]{2,1,0:T(8,128)}, u32[]{:S(2)}) copy-start(f32[8,8,192]{2,1,0:T(8,128)} %get-tuple-element.140) | copy-start | bytes 147460
  409.4 35.8 %copy-start.83 = (f32[8,8,192]{2,1,0:T(8,128)S(1)}, f32[8,8,192]{2,1,0:T(8,128)}, u32[]{:S(2)}) copy-start(f32[8,8,192]{2,1,0:T(8,128)} %get-tuple-element.142) | copy-start | bytes 147460
  409.4 35.8 %copy-start.193 = (pred[192]{0:T(512)(128)(4,1)S(1)}, pred[192]{0:T(512)(128)(4,1)}, u32[]{:S(2)}) copy-start(pred[192]{0:T(512)(128)(4,1)} %copy-done.191) | copy-start | bytes 580
  409.4 35.8 %copy-start.203 = (pred[191]{0:T(512)(128)(4,1)S(1)}, pred[191]{0:T(512)(128)(4,1)}, u32[]{:S(2)}) copy-start(pred[191]{0:T(512)(128)(4,1)} %slice.447) | copy-start | bytes 577
  445.0 9.8 %copy-start.198 = (f32[256]{0:T(256)S(1)}, f32[256]{0:T(256)}, u32[]{:S(2)}) copy-start(f32[256]{0:T(256)} %get-tuple-element.16) | copy-start | bytes 3076
  445.0 9.8 %copy-start.200 = (f32[256]{0:T(256)S(1)}, f32[256]{0:T(256)}, u32[]{:S(2)}) copy-start(f32[256]{0:T(256)} %get-tuple-element.14) | copy-start | bytes 3076
  445.9 116.1 %copy-start.195 = (pred[8]{0:T(512)(128)(4,1)S(1)}, pred[8]{0:T(512)(128)(4,1)}, u32[]{:S(2)}) copy-start(pred[8]{0:T(512)(128)(4,1)} %constant.73.clone.1) | copy-start | bytes 28
  446.0 104.8 %collective-permute-start.13 = (f32[4,16,192]{2,1,0:T(8,128)S(1)}, f32[4,16,192]{2,1,0:T(8,128)S(1)}, u32[]{:S(2)}, u32[]{:S(2)}) collective-permute-start(f32[4,16,192]{2,1,0:T(8,128)S(1)} %get-tuple-element.119), channel_id=1, source_target_pairs={{16,0},{32,16},{48,32},{64,48},{80,64},{96,80},{112,96},{128,112},... | collective-permute-start | bytes 147464 | tf_op jit(solution)/shard_map/ppermute | solution.py:23
  452.8 98.0 %collective-permute-start.12 = (f32[4,16,192]{2,1,0:T(8,128)S(1)}, f32[4,16,192]{2,1,0:T(8,128)S(1)}, u32[]{:S(2)}, u32[]{:S(2)}) collective-permute-start(f32[4,16,192]{2,1,0:T(8,128)S(1)} %get-tuple-element.118), channel_id=1, source_target_pairs={{0,16},{16,32},{32,48},{48,64},{64,80},{80,96},{96,112},{112,128},... | collective-permute-start | bytes 147464 | tf_op jit(solution)/shard_map/ppermute | solution.py:22
  550.8 4.9 collective-permute-start.15
  552.8 9.1 %collective-permute-start.14 = (f32[24,4,192]{2,1,0:T(4,128)S(1)}, f32[24,4,192]{2,1,0:T(4,128)S(1)}, u32[]{:S(2)}, u32[]{:S(2)}) collective-permute-start(f32[24,4,192]{2,1,0:T(4,128)S(1)} %get-tuple-element.114), channel_id=1, source_target_pairs={{0,1},{1,2},{2,3},{3,4},{4,5},{5,6},{6,7},{7,8},{8,9},{9,10},{10,1... | collective-permute-start | bytes 221192 | tf_op jit(solution)/shard_map/ppermute | solution.py:22
  (174 other events, 564.2 us)
Sparse Core Ops, SparseCore 0:
  291.4 153.4 all-reduce.81
  448.3 284.9 all-reduce.79
